TPU v7x, 32 devices: a whole 2x2x4 slice. The times are simulated.
32 devices in a mesh: gx: 4 (over z), gy: 4 (over x, core), col: 2 (over y).
Axes of the slice: x: 2, y: 2, z: 4, core: 2. Of those that a mesh axis runs over, the one named last changes fastest.
Arguments:
- fields: bfloat16 [2, 128, 128, 32, 128], P('col', 'gx', 'gy'), may hold values from -6 to 6
- spectral: bfloat16 [1, 16, 16, 2, 32, 32, 16], P(None, 'gx', 'gy', None, None, 'col'), may hold values from -0.75 to 0.75
- skip_weight: bfloat16 [1, 32, 32], replicated, may hold values from -1 to 1
- skip_bias: float32 [1, 32], replicated, may hold values from -3 to 3
- norm_gain: float32 [1, 32], replicated, may hold values from 0.5 to 1.5
- norm_shift: float32 [1, 32], replicated, may hold values from -3 to 3
Outputs:
- activations: bfloat16 [2, 128, 128, 32, 128], P('col', 'gx', 'gy')
All inputs are finite; a program needn't handle non-finite values.
Results may differ from a plain program's by a relative error of at most 0.012.
Values may be sent and summed in bfloat16 or wider, within the bound.
A program may use at most 128 MiB of HBM per device.

v0:
```python
import math
import jax
import jax.numpy as jnp
from jax import lax
from jax.sharding import PartitionSpec as P

X = 128
Y = 128
Z = 128
MX = 16
MY = 16
MZ = 16
norm_eps = 1e-05


def signed_freqs(count):
    index = jnp.arange(count, dtype=jnp.int32)
    return jnp.where(index < count // 2, index, index - count)


def angles(positions, frequency, length):
    turn_count = positions[:, None] * frequency[None, :] % length
    return turn_count.astype(jnp.float32) * (2.0 * math.pi / length)


def forward_table(positions, frequency, length, factor):
    phase_angle = angles(positions, frequency, length)
    cosine = jnp.cos(phase_angle) * factor
    sine_part = jnp.sin(phase_angle) * factor
    from_real = jnp.stack([cosine, -sine_part], axis=-1)
    from_imag = jnp.stack([sine_part, cosine], axis=-1)
    return jnp.stack([from_real, from_imag], axis=1)


def inverse_table(frequency, positions, length):
    phase_angle = angles(positions, frequency, length).T
    cosine = jnp.cos(phase_angle)
    sine_part = jnp.sin(phase_angle)
    from_real = jnp.stack([cosine, sine_part], axis=-1)
    from_imag = jnp.stack([-sine_part, cosine], axis=-1)
    return jnp.stack([from_real, from_imag], axis=1)


def depth_tables(length, count):
    frequency = jnp.arange(count, dtype=jnp.int32)
    phase_angle = angles(jnp.arange(length, dtype=jnp.int32), frequency, length)
    forward = jnp.concatenate([jnp.cos(phase_angle), -jnp.sin(phase_angle)], axis=1)
    backward = jnp.concatenate([jnp.cos(phase_angle).T, -jnp.sin(phase_angle).T], axis=0)
    return (forward.astype(jnp.bfloat16), backward.astype(jnp.bfloat16))


def mix_modes(spectrum, weight):

    def contract(left, right):
        return jnp.einsum("abcz,abcdz->abdz", left, right, preferred_element_type=jnp.float32)

    real_in = spectrum[:, :, :, 0]
    imag_in = spectrum[:, :, :, 1]
    real_weight = weight[:, :, 0]
    imag_weight = weight[:, :, 1]
    real_out = contract(real_in, real_weight) - contract(imag_in, imag_weight)
    imag_out = contract(real_in, imag_weight) + contract(imag_in, real_weight)
    return jnp.stack([real_out, imag_out], axis=3)


def finish(spectral_part, skip_part, offset, scaling, shift_term):
    pre_norm = spectral_part + skip_part + offset[:, None]
    centre = jnp.mean(pre_norm, axis=2, keepdims=True)
    spread = jnp.mean(jnp.square(pre_norm - centre), axis=2, keepdims=True)
    normed = (pre_norm - centre) * lax.rsqrt(spread + norm_eps) * scaling[:, None] + shift_term[
        :, None
    ]
    return jax.nn.gelu(normed, approximate=False).astype(jnp.bfloat16)


def local(fields, spectral, skip_weight, skip_bias, norm_gain, norm_shift):
    highest = lax.Precision.HIGHEST
    hidden = fields[0]
    tile_first, tile_second, channels, depth_cells = hidden.shape
    first_cells = lax.axis_index("gx") * tile_first + jnp.arange(tile_first, dtype=jnp.int32)
    second_cells = lax.axis_index("gy") * tile_second + jnp.arange(tile_second, dtype=jnp.int32)
    depth_forward, depth_backward = depth_tables(Z, MZ)
    second_forward = forward_table(second_cells, signed_freqs(MY), Y, 1.0).astype(jnp.bfloat16)
    first_forward = forward_table(first_cells, signed_freqs(MX), X, 1.0 / math.sqrt(X * Y * Z))
    first_inverse = inverse_table(signed_freqs(MX), first_cells, X).astype(jnp.bfloat16)
    second_inverse = inverse_table(signed_freqs(MY), second_cells, Y)
    inverse_scale = 1.0 / math.sqrt(MX * MY * MZ)
    amplitude = jnp.dot(
        hidden.reshape(-1, depth_cells), depth_forward, preferred_element_type=jnp.float32
    )
    amplitude = amplitude.astype(jnp.bfloat16).reshape(tile_first, tile_second, channels, 2, MZ)
    along_second = jnp.einsum(
        "xycrz,yrks->xkcsz", amplitude, second_forward, preferred_element_type=jnp.float32
    )
    summed_second = lax.psum_scatter(
        along_second.astype(jnp.bfloat16), "gy", scatter_dimension=1, tiled=True
    ).astype(jnp.float32)
    partial_modes = jnp.einsum("xkcsz,xsjt->jkctz", summed_second, first_forward, precision=highest)
    summed = lax.psum_scatter(
        partial_modes.astype(jnp.bfloat16), "gx", scatter_dimension=0, tiled=True
    )
    weights_here = spectral[0]
    mixed_modes = mix_modes(summed, lax.all_gather(weights_here, "col", axis=4, tiled=True)).astype(
        jnp.bfloat16
    )
    gathered_second = lax.all_gather(mixed_modes, "gy", axis=1, tiled=True)
    full_modes = lax.all_gather(gathered_second, "gx", axis=0, tiled=True)
    rows_first = jnp.einsum(
        "jkcsz,jsxt->xkctz", full_modes, first_inverse, preferred_element_type=jnp.float32
    )
    rows_both = jnp.einsum(
        "xkcsz,ksyt->xyctz", rows_first, second_inverse, precision=highest
    ).astype(jnp.bfloat16)
    spectral_part = jnp.dot(
        rows_both.reshape(-1, 2 * MZ), depth_backward, preferred_element_type=jnp.float32
    )
    spectral_part = (
        spectral_part.reshape(tile_first, tile_second, channels, depth_cells) * inverse_scale
    )
    skip_part = jnp.einsum(
        "oc,xycz->xyoz", skip_weight[0], hidden, preferred_element_type=jnp.float32
    )
    hidden = finish(spectral_part, skip_part, skip_bias[0], norm_gain[0], norm_shift[0])
    return hidden[None]


def solution(mesh):
    placed = (
        P("col", "gx", "gy", None, None),
        P(None, "gx", "gy", None, None, "col", None),
        P(),
        P(),
        P(),
        P(),
    )
    return jax.shard_map(
        local,
        mesh=mesh,
        in_specs=placed,
        out_specs=P("col", "gx", "gy", None, None),
        check_vma=False,
    )
```

profile of v0, /device:TPU:0, one launch (start us, length us, event | category | flops | bytes accessed | tf_op | source)
XLA Modules:
  0.0 268.1 jit_solution(5952482807343169716)
XLA Ops:
  7.4 0.0 copy-start
  7.4 0.0 reduce-scatter.3.cloned.1.call-start
  7.4 0.1 negate_convert_fusion.1
  7.4 6.4 %fusion = bf16[32768,32]{0,1:T(8,128)(2,1)S(1)} fusion(bf16[32768,128]{1,0:T(8,128)(2,1)} %bitcast.159, bf16[128,16]{0,1:T(8,128)(2,1)S(1)} %get-tuple-element.37, bf16[128,16]{0,1:T(8,128)(2,1)S(1)} %get-tuple-element.38), kind=kOutput, calls=%fused_computation.1 | convolution fusion | flops 269500416 | bytes 10493952 | tf_op jit(solution)/shard_map/dot_general | solution.py:88
  13.8 7.9 %reshape.722 = bf16[32,32,32,2,16]{2,1,0,4,3:T(8,128)(2,1)} reshape(bf16[32768,32]{0,1:T(8,128)(2,1)S(1)} %fusion) | data formatting | bytes 4194304 | tf_op jit(solution)/shard_map/reshape | solution.py:91
  21.7 0.2 fusion.88
  21.9 4.7 %fusion.24 = bf16[32,16,32,2,16]{2,1,4,0,3:T(8,128)(2,1)S(1)} fusion(bf16[32,32,32,2,16]{2,1,0,4,3:T(8,128)(2,1)} %reshape.722, bf16[32,1,16,2]{0,2,1,3:T(8,128)(2,1)S(1)} %get-tuple-element.16, bf16[32,1,16,2]{0,2,1,3:T(8,128)(2,1)S(1)} %get-tuple-element.15), kind=kOutput, calls=%fused_computation.37 | convolution fusion | flops 67641344 | bytes 3149824 | tf_op jit(solution)/shard_map/xycrz,yrks->xkcsz/dot_general | solution.py:92
  26.6 3.1 %copy.26 = bf16[32,16,32,2,16]{2,4,3,0,1:T(8,128)(2,1)} copy(bf16[32,16,32,2,16]{2,1,4,0,3:T(8,128)(2,1)S(1)} %fusion.24) | data formatting | bytes 2097152 | tf_op jit(solution)/shard_map/convert_element_type | solution.py:96
  29.7 0.0 reduce-scatter.3.cloned.1.call-update
  29.7 0.0 all-gather.3.cloned.1.call-start
  29.8 0.5 all-gather.3.cloned.1.call-update
  30.3 0.2 reduce-scatter.5.cloned.1.call-start
  30.5 0.1 negate_convert_fusion
  30.6 0.2 fusion.85
  30.8 0.0 copy-done
  30.8 15.1 %fusion.13 = f32[32,32,128,32]{2,3,1,0:T(8,128)} fusion(bf16[1,32,32,32,128]{4,3,2,1,0:T(8,128)(2,1)} %param.6, bf16[1,32,32]{2,1,0:T(8,128)(2,1)S(1)} %copy-done), kind=kOutput, calls=%fused_computation.27 | convolution fusion | flops 268435456 | bytes 25167872 | tf_op jit(solution)/shard_map/oc,xycz->xyoz/dot_general | solution.py:120
  46.0 31.2 %reduce-scatter.3.cloned.1.call-done = bf16[32,4,32,2,16]{2,4,3,0,1:T(8,128)(2,1)} async-done(((bf16[32,16,32,2,16]{2,4,3,0,1:T(8,128)(2,1)}), bf16[32,4,32,2,16]{2,4,3,0,1:T(8,128)(2,1)}) %reduce-scatter.3.cloned.1.call-update) | async-done | bytes 262160 | tf_op jit(solution)/shard_map/reduce_scatter | solution.py:95
  77.2 1.9 fusion.30
  79.1 0.9 copy.29
  80.1 0.0 reduce-scatter.5.cloned.1.call-update
  80.1 11.0 %all-gather.3.cloned.1.call-done = bf16[1,4,4,2,32,32,16]{4,6,5,3,2,1,0:T(8,128)(2,1)} async-done(((bf16[1,4,4,2,32,16,16]{4,6,5,3,2,1,0:T(8,128)(2,1)}), bf16[1,4,4,2,32,32,16]{4,6,5,3,2,1,0:T(8,128)(2,1)}) %all-gather.3.cloned.1.call-update) | async-done | bytes 1048592 | tf_op jit(solution)/shard_map/all_gather | solution.py:103
  91.1 4.5 %slice_bitcast_fusion = (bf16[4,4,32,32,16]{2,4,3,1,0:T(8,128)(2,1)}, bf16[4,4,32,32,16]{2,4,3,1,0:T(8,128)(2,1)S(1)}) fusion(bf16[4,4,2,32,32,16]{3,5,4,2,1,0:T(8,128)(2,1)} %bitcast.161), kind=kLoop, calls=%fused_computation.39 | loop fusion | bytes 2097152 | tf_op jit(solution)/shard_map/squeeze | solution.py:60
  95.6 4.5 %copy.44 = bf16[4,4,32,32,16]{3,2,4,1,0:T(8,128)(2,1)} copy(bf16[4,4,32,32,16]{2,4,3,1,0:T(8,128)(2,1)} %get-tuple-element.5) | data formatting | bytes 1048576 | tf_op jit(solution)/shard_map/squeeze | solution.py:60
  100.2 2.9 %copy.41 = bf16[4,4,32,32,16]{3,2,4,1,0:T(8,128)(2,1)} copy(bf16[4,4,32,32,16]{2,4,3,1,0:T(8,128)(2,1)S(1)} %get-tuple-element.6) | data formatting | bytes 1048576 | tf_op jit(solution)/shard_map/squeeze | solution.py:59
  103.1 0.0 reduce-scatter.5.cloned.1.call-done
  103.1 0.9 slice_bitcast_fusion.3
  104.0 2.2 fusion.39
  106.2 2.3 fusion.37
  108.5 2.3 fusion.35
  110.7 2.2 fusion.41
  113.1 7.2 %all_gather.10 = bf16[4,16,32,2,16]{2,4,3,0,1:T(8,128)(2,1)S(1)} all-gather(bf16[4,4,32,2,16]{2,4,3,0,1:T(8,128)(2,1)S(1)} %pad_maximum_fusion), channel_id=1, replica_groups=mesh['gx'=4,'gy'=4,'col'=2] {'gy'}, dimensions={1}, use_global_device_ids=true | all-gather | bytes 163840 | tf_op jit(solution)/shard_map/all_gather | solution.py:106
  120.3 38.6 %all_gather.11 = bf16[16,16,32,2,16]{2,4,3,1,0:T(8,128)(2,1)S(1)} all-gather(bf16[4,16,32,2,16]{2,4,3,1,0:T(8,128)(2,1)S(1)} %copy.30), channel_id=1, replica_groups=mesh['gx'=4,'gy'=4,'col'=2] {'gx'}, dimensions={0}, use_global_device_ids=true | all-gather | bytes 655360 | tf_op jit(solution)/shard_map/all_gather | solution.py:107
  158.8 1.5 convolution_bitcast_fusion
  160.3 0.0 copy-start.4
  160.3 22.8 %fusion.12 = bf16[32,32,32,2,16]{2,1,4,0,3:T(8,128)(2,1)} fusion(f32[32,16,32,2,16]{2,0,4,1,3:T(8,128)S(1)} %convolution_bitcast_fusion, f32[16,1,32,2]{2,0,3,1:T(8,128)S(1)} %get-tuple-element.10, f32[16,1,32,2]{2,0,3,1:T(8,128)S(1)} %get-tuple-element.9), kind=kOutput, calls=%fused_computation.26 | convolution fusion | flops 403703808 | bytes 4202496 | tf_op jit(solution)/shard_map/xkcsz,ksyt->xyctz/dot_general | solution.py:111
  183.1 10.5 %copy.34 = bf16[32,32,32,2,16]{2,4,3,1,0:T(8,128)(2,1)} copy(bf16[32,32,32,2,16]{2,1,4,0,3:T(8,128)(2,1)} %fusion.12) | data formatting | bytes 4194304 | tf_op jit(solution)/shard_map/convert_element_type | solution.py:113
  193.6 0.0 copy-done.4
  193.6 14.5 %fusion.93 = (f32[32,32,128]{2,1,0:T(8,128)S(1)}, f32[32,32,32,128]{3,2,1,0:T(8,128)}) fusion(f32[32]{0:T(128)S(1)} %bitcast.164, f32[32,32,128,32]{2,3,1,0:T(8,128)} %fusion.13, bf16[32,32,32,32]{2,3,1,0:T(8,128)(2,1)} %bitcast.160, bf16[16,128]{1,0:T(8,128)(2,1)S(1)} %get-tuple-element.41, bf16[16,128]{1,0:T(8,128)(2,1)S(1)} %get-tuple-element.42), kind=kOutput, calls=%fused_computation.167 | convolution fusion | flops 285097984 | bytes 36184192 | tf_op jit(solution)/shard_map/dot_general | solution.py:114
  208.1 0.0 copy-start.2
  208.1 0.0 copy-start.3
  208.2 0.0 copy-start.1
  208.2 10.9 %multiply_reduce_fusion = f32[32,32,128]{2,1,0:T(8,128)S(1)} fusion(f32[32,32,32,128]{3,2,1,0:T(8,128)} %get-tuple-element.36, f32[32,32,128]{2,1,0:T(8,128)S(1)} %broadcast_multiply_fusion), kind=kLoop, calls=%fused_computation.23 | loop fusion | flops 12451840 | bytes 17825792 | tf_op jit(solution)/shard_map/reduce_sum | solution.py:69
  219.1 0.1 add_rsqrt_fusion
  219.2 0.0 copy-done.2
  219.2 0.0 copy-done.3
  219.2 41.4 %fusion.21 = bf16[1,32,32,32,128]{4,3,2,1,0:T(8,128)(2,1)} fusion(f32[32]{0:T(128)S(1)} %bitcast.162, f32[32]{0:T(128)S(1)} %bitcast.163, f32[32,32,128]{2,1,0:T(8,128)S(1)} %add_rsqrt_fusion, f32[32,32,32,128]{3,2,1,0:T(8,128)} %get-tuple-element.36, f32[32,32,128]{2,1,0:T(8,128)S(1)} %broadcast_multiply_fusion), kind=kLoop, calls=%fused_computation.36 | loop fusion | flops 289406976 | bytes 26214656 | tf_op jit(solution)/shard_map/broadcast_in_dim | solution.py:124
  260.6 0.0 copy-done.1
  (11 shorter events, 0.2 us)
Async XLA Ops:
  7.4 23.4 %copy-start = (bf16[1,32,32]{2,1,0:T(8,128)(2,1)S(1)}, bf16[1,32,32]{2,1,0:T(8,128)(2,1)}, u32[]{:S(2)}) copy-start(bf16[1,32,32]{2,1,0:T(8,128)(2,1)} %param.8) | copy-start | bytes 6148
  7.4 69.8 %reduce-scatter.3.cloned.1.call-start = ((), (), s32[]{:S(2)}) async-start(), calls=%async_computation.2 | async-start | bytes 5242880 | tf_op jit(solution)/shard_map/reduce_scatter | solution.py:95
  29.7 61.4 %all-gather.3.cloned.1.call-start = ((), (), s32[]{:S(2)}) async-start(), calls=%async_computation.4 | async-start | bytes 6291456 | tf_op jit(solution)/shard_map/all_gather | solution.py:103
  30.3 72.8 %reduce-scatter.5.cloned.1.call-start = ((), (), s32[]{:S(2)}) async-start(), calls=%async_computation.3 | async-start | bytes 655360 | tf_op jit(solution)/shard_map/reduce_scatter | solution.py:99
  160.3 33.3 %copy-start.4 = (f32[1,32]{1,0:T(1,128)S(1)}, f32[1,32]{1,0:T(1,128)}, u32[]{:S(2)}) copy-start(f32[1,32]{1,0:T(1,128)} %param.9) | copy-start | bytes 388
  208.1 11.1 %copy-start.2 = (f32[1,32]{1,0:T(1,128)S(1)}, f32[1,32]{1,0:T(1,128)}, u32[]{:S(2)}) copy-start(f32[1,32]{1,0:T(1,128)} %param.11) | copy-start | bytes 388
  208.1 11.1 %copy-start.3 = (f32[1,32]{1,0:T(1,128)S(1)}, f32[1,32]{1,0:T(1,128)}, u32[]{:S(2)}) copy-start(f32[1,32]{1,0:T(1,128)} %param.10) | copy-start | bytes 388
  208.2 52.5 %copy-start.1 = (bf16[1,32,32]{2,1,0:T(8,128)(2,1)S(1)}, bf16[1,32,32]{2,1,0:T(8,128)(2,1)}, u32[]{:S(2)}) copy-start(bf16[1,32,32]{2,1,0:T(8,128)(2,1)} %param.8) | copy-start | bytes 6148
Sparse Core Ops, SparseCore 0:
  29.9 47.2 reduce-scatter.2
  80.2 21.8 reduce-scatter.4
Sparse Core Ops, SparseCore 1:
  31.8 59.3 all-gather.2
where the time goes:
time: 269 us; the launch traced here: 268 us
  matrix products  75.9 us (28%)
  other arithmetic  53 us (20%)
  blocking collectives  45.7 us (17%)
  waiting for transfers between devices  42.8 us (16%)
  local copies, waits for them, and re-layouts  35.4 us (13%)
  between operations  15 us (6%)
    broadcast_in_dim x1, other arithmetic, local(): return hidden[None]  41.4 us
    all_gather x1, blocking collectives, local(): full_modes = lax.all_gather(gathered_second, 'gx', axis=0, tiled=True)  38.6 us
    reduce_scatter x1, waiting for transfers between devices, local(): lax.psum_scatter(along_second.astype(jnp.bfloat16), 'gy', scatter_dimensi...  31.2 us
    dot_general x1, matrix products, local(): jnp.einsum('xkcsz,ksyt->xyctz', rows_first, second_inverse, precision=hig...  22.8 us
    dot_general x1, matrix products, local(): jnp.einsum('oc,xycz->xyoz', skip_weight[0], hidden, preferred_element_typ...  15.1 us
    dot_general x1, matrix products, local(): jnp.dot(rows_both.reshape(-1, 2 * MZ), depth_backward, preferred_element_...  14.5 us
    all_gather x1, waiting for transfers between devices, local(): lax.all_gather(weights_here, 'col', axis=4, tiled=True)  11 us
    reduce_sum x1, other arithmetic, finish(): spread = jnp.mean(jnp.square(pre_norm - centre), axis=2, keepdims=True)  10.9 us
  transfers between devices with their start and end apart: 3, of which 2 were waited for; matrix products, arithmetic and copies ran while one was open for 11% of the time, Pallas kernels for 0%

commit v1 on v0

--- a/solution.py
+++ b/solution.py
@@ -11,6 +11,16 @@
 MY = 16
 MZ = 16
 norm_eps = 1e-05
+
+
+def pass_along(x, name, d):
+    n_dev = lax.axis_size(name)
+    block, tiles = (x, [x])
+    for _ in range(n_dev - 1):
+        block = lax.ppermute(block, name, [(i, (i + 1) % n_dev) for i in range(n_dev)])
+        tiles.insert(0, block)
+    row_of_blocks = jnp.concatenate(tiles, axis=d)
+    return jnp.roll(row_of_blocks, (lax.axis_index(name) + 1) * x.shape[d], axis=d)
 
 
 def signed_freqs(count):
@@ -104,7 +114,7 @@
         jnp.bfloat16
     )
     gathered_second = lax.all_gather(mixed_modes, "gy", axis=1, tiled=True)
-    full_modes = lax.all_gather(gathered_second, "gx", axis=0, tiled=True)
+    full_modes = pass_along(gathered_second, "gx", 0)
     rows_first = jnp.einsum(
         "jkcsz,jsxt->xkctz", full_modes, first_inverse, preferred_element_type=jnp.float32
     )

time: 269 us -> 290 us (1.078)
  waiting for transfers between devices: 42.8 us -> 90.5 us
  blocking collectives: 45.7 us -> 7.15 us
  local copies, waits for them, and re-layouts: 35.4 us -> 48 us
    all_gather x1 -> x0, blocking collectives: 38.6 us -> none  [local(): full_modes = lax.all_gather(gathered_second, 'gx', axis=0, tiled=True)]
    ppermute x0 -> x3, waiting for transfers between devices: none -> 32.1 us  [pass_along(): lax.ppermute(block, name, [(i, (i + 1) % n_dev) for i in range(n_dev)])]
    reduce_scatter x1, waiting for transfers between devices: 31.2 us -> 46.8 us  [local(): lax.psum_scatter(along_second.astype(jnp.bfloat16), 'gy', scatter_dimensi...]
    concatenate x0 -> x1, local copies, waits for them, and re-layouts: none -> 12.3 us  [pass_along(): jnp.roll(row_of_blocks, (lax.axis_index(name) + 1) * x.shape[d], axis=d)]
    dot_general x1, matrix products: 15.1 us -> 11.5 us  [local(): jnp.einsum('oc,xycz->xyoz', skip_weight[0], hidden, preferred_element_typ...]
  transfers between devices with their start and end apart: 3 -> 6, of which waited for: 2 -> 5; matrix products, arithmetic and copies ran while one was open for 11% -> 9% of each run, Pallas kernels for 0% -> 0%
where the time goes in v1:
time: 290 us; the launch traced here: 289 us
  waiting for transfers between devices  90.5 us (31%)
  matrix products  73.8 us (25%)
  other arithmetic  53 us (18%)
  local copies, waits for them, and re-layouts  48 us (17%)
  between operations  15 us (5%)
  blocking collectives  7.15 us (2%)
    reduce_scatter x1, waiting for transfers between devices, local(): lax.psum_scatter(along_second.astype(jnp.bfloat16), 'gy', scatter_dimensi...  46.8 us
    broadcast_in_dim x1, other arithmetic, local(): return hidden[None]  41.4 us
    ppermute x3, waiting for transfers between devices, pass_along(): lax.ppermute(block, name, [(i, (i + 1) % n_dev) for i in range(n_dev)])  32.1 us
    dot_general x1, matrix products, local(): jnp.einsum('xkcsz,ksyt->xyctz', rows_first, second_inverse, precision=hig...  22.8 us
    dot_general x1, matrix products, local(): jnp.dot(rows_both.reshape(-1, 2 * MZ), depth_backward, preferred_element_...  14.5 us
    concatenate x1, local copies, waits for them, and re-layouts, pass_along(): jnp.roll(row_of_blocks, (lax.axis_index(name) + 1) * x.shape[d], axis=d)  12.3 us
    dot_general x1, matrix products, local(): jnp.einsum('oc,xycz->xyoz', skip_weight[0], hidden, preferred_element_typ...  11.5 us
    all_gather x1, waiting for transfers between devices, local(): lax.all_gather(weights_here, 'col', axis=4, tiled=True)  11 us
  transfers between devices with their start and end apart: 6, of which 5 were waited for; matrix products, arithmetic and copies ran while one was open for 9% of the time, Pallas kernels for 0%

profile of v1, /device:TPU:0, one launch (start us, length us, event | category | flops | bytes accessed | tf_op | source)
XLA Modules:
  0.0 289.3 jit_solution(12933285335189747278)
XLA Ops:
  7.4 0.0 copy-start
  7.4 0.0 reduce-scatter.3.cloned.1.call-start
  7.4 0.1 negate_convert_fusion.1
  7.4 6.4 %fusion = bf16[32768,32]{0,1:T(8,128)(2,1)S(1)} fusion(bf16[32768,128]{1,0:T(8,128)(2,1)} %bitcast.159, bf16[128,16]{0,1:T(8,128)(2,1)S(1)} %get-tuple-element.37, bf16[128,16]{0,1:T(8,128)(2,1)S(1)} %get-tuple-element.38), kind=kOutput, calls=%fused_computation.1 | convolution fusion | flops 269500416 | bytes 10493952 | tf_op jit(solution)/shard_map/dot_general | solution.py:98
  13.8 7.9 %reshape.722 = bf16[32,32,32,2,16]{2,1,0,4,3:T(8,128)(2,1)} reshape(bf16[32768,32]{0,1:T(8,128)(2,1)S(1)} %fusion) | data formatting | bytes 4194304 | tf_op jit(solution)/shard_map/reshape | solution.py:101
  21.7 0.2 fusion.88
  21.9 4.7 %fusion.24 = bf16[32,16,32,2,16]{2,1,4,0,3:T(8,128)(2,1)S(1)} fusion(bf16[32,32,32,2,16]{2,1,0,4,3:T(8,128)(2,1)} %reshape.722, bf16[32,1,16,2]{0,2,1,3:T(8,128)(2,1)S(1)} %get-tuple-element.16, bf16[32,1,16,2]{0,2,1,3:T(8,128)(2,1)S(1)} %get-tuple-element.15), kind=kOutput, calls=%fused_computation.37 | convolution fusion | flops 67641344 | bytes 3149824 | tf_op jit(solution)/shard_map/xycrz,yrks->xkcsz/dot_general | solution.py:102
  26.6 3.1 %copy.26 = bf16[32,16,32,2,16]{2,4,3,0,1:T(8,128)(2,1)} copy(bf16[32,16,32,2,16]{2,1,4,0,3:T(8,128)(2,1)S(1)} %fusion.24) | data formatting | bytes 2097152 | tf_op jit(solution)/shard_map/convert_element_type | solution.py:106
  29.7 0.0 reduce-scatter.3.cloned.1.call-update
  29.7 0.0 all-gather.3.cloned.1.call-start
  29.8 0.5 all-gather.3.cloned.1.call-update
  30.3 0.0 reduce-scatter.5.cloned.1.call-start
  30.4 46.8 %reduce-scatter.3.cloned.1.call-done = bf16[32,4,32,2,16]{2,4,3,0,1:T(8,128)(2,1)} async-done(((bf16[32,16,32,2,16]{2,4,3,0,1:T(8,128)(2,1)}), bf16[32,4,32,2,16]{2,4,3,0,1:T(8,128)(2,1)}) %reduce-scatter.3.cloned.1.call-update) | async-done | bytes 262160 | tf_op jit(solution)/shard_map/reduce_scatter | solution.py:105
  77.2 1.9 fusion.30
  79.1 0.9 copy.29
  80.1 0.0 reduce-scatter.5.cloned.1.call-update
  80.1 11.0 %all-gather.3.cloned.1.call-done = bf16[1,4,4,2,32,32,16]{4,6,5,3,2,1,0:T(8,128)(2,1)} async-done(((bf16[1,4,4,2,32,16,16]{4,6,5,3,2,1,0:T(8,128)(2,1)}), bf16[1,4,4,2,32,32,16]{4,6,5,3,2,1,0:T(8,128)(2,1)}) %all-gather.3.cloned.1.call-update) | async-done | bytes 1048592 | tf_op jit(solution)/shard_map/all_gather | solution.py:113
  91.1 4.5 %slice_bitcast_fusion = (bf16[4,4,32,32,16]{2,4,3,1,0:T(8,128)(2,1)}, bf16[4,4,32,32,16]{2,4,3,1,0:T(8,128)(2,1)S(1)}) fusion(bf16[4,4,2,32,32,16]{3,5,4,2,1,0:T(8,128)(2,1)} %bitcast.161), kind=kLoop, calls=%fused_computation.39 | loop fusion | bytes 2097152 | tf_op jit(solution)/shard_map/squeeze | solution.py:70
  95.6 4.5 %copy.45 = bf16[4,4,32,32,16]{3,2,4,1,0:T(8,128)(2,1)} copy(bf16[4,4,32,32,16]{2,4,3,1,0:T(8,128)(2,1)} %get-tuple-element.5) | data formatting | bytes 1048576 | tf_op jit(solution)/shard_map/squeeze | solution.py:70
  100.2 2.9 %copy.42 = bf16[4,4,32,32,16]{3,2,4,1,0:T(8,128)(2,1)} copy(bf16[4,4,32,32,16]{2,4,3,1,0:T(8,128)(2,1)S(1)} %get-tuple-element.6) | data formatting | bytes 1048576 | tf_op jit(solution)/shard_map/squeeze | solution.py:69
  103.1 0.9 slice_bitcast_fusion.3
  104.0 2.2 fusion.39
  106.2 2.3 fusion.37
  108.5 2.2 fusion.35
  110.7 2.3 fusion.41
  113.1 7.2 %all_gather.7 = bf16[4,16,32,2,16]{2,4,3,0,1:T(8,128)(2,1)S(1)} all-gather(bf16[4,4,32,2,16]{2,4,3,0,1:T(8,128)(2,1)S(1)} %pad_maximum_fusion), channel_id=1, replica_groups=mesh['gx'=4,'gy'=4,'col'=2] {'gy'}, dimensions={1}, use_global_device_ids=true | all-gather | bytes 163840 | tf_op jit(solution)/shard_map/all_gather | solution.py:116
  120.2 0.3 copy.30
  120.5 1.7 collective-permute-start
  122.2 11.5 %fusion.13 = f32[32,32,128,32]{2,3,1,0:T(8,128)} fusion(bf16[1,32,32,32,128]{4,3,2,1,0:T(8,128)(2,1)} %param.6, bf16[1,32,32]{2,1,0:T(8,128)(2,1)S(1)} %copy-done), kind=kOutput, calls=%fused_computation.27 | convolution fusion | flops 268435456 | bytes 25167872 | tf_op jit(solution)/shard_map/oc,xycz->xyoz/dot_general | solution.py:130
  133.7 3.0 %collective-permute-done = bf16[4,16,32,2,16]{2,0,3,4,1:T(4,128)(2,1)S(1)} collective-permute-done((bf16[4,16,32,2,16]{2,0,3,4,1:T(4,128)(2,1)S(1)}, bf16[4,16,32,2,16]{2,0,3,4,1:T(4,128)(2,1)S(1)}, u32[]{:S(2)}, u32[]{:S(2)}) %collective-permute-start) | collective-permute-done | bytes 131104 | tf_op jit(solution)/shard_map/ppermute | solution.py:20
  136.7 0.0 collective-permute-start.1
  136.7 0.2 fusion.85
  136.9 14.9 %collective-permute-done.1 = bf16[4,16,32,2,16]{2,0,3,4,1:T(4,128)(2,1)S(1)} collective-permute-done((bf16[4,16,32,2,16]{2,0,3,4,1:T(4,128)(2,1)S(1)}, bf16[4,16,32,2,16]{2,0,3,4,1:T(4,128)(2,1)S(1)}, u32[]{:S(2)}, u32[]{:S(2)}) %collective-permute-start.1) | collective-permute-done | bytes 131104 | tf_op jit(solution)/shard_map/ppermute | solution.py:20
  151.8 0.0 collective-permute-start.2
  151.9 0.1 negate_convert_fusion
  151.9 14.2 %collective-permute-done.2 = bf16[4,16,32,2,16]{2,0,3,4,1:T(4,128)(2,1)S(1)} collective-permute-done((bf16[4,16,32,2,16]{2,0,3,4,1:T(4,128)(2,1)S(1)}, bf16[4,16,32,2,16]{2,0,3,4,1:T(4,128)(2,1)S(1)}, u32[]{:S(2)}, u32[]{:S(2)}) %collective-permute-start.2) | collective-permute-done | bytes 131104 | tf_op jit(solution)/shard_map/ppermute | solution.py:20
  166.1 12.3 %concatenate.15 = bf16[32,16,32,2,16]{2,0,3,4,1:T(8,128)(2,1)} concatenate(bf16[4,16,32,2,16]{2,0,3,4,1:T(4,128)(2,1)S(1)} %collective-permute-done.2, bf16[4,16,32,2,16]{2,0,3,4,1:T(4,128)(2,1)S(1)} %collective-permute-done.1, bf16[4,16,32,2,16]{2,0,3,4,1:T(4,128)(2,1)S(1)} %collective-permute-done, bf16[4,16,32,2,16]{2,0,3,4,1:T(4,128)(2,1)S(1)} %copy.30, ...), dimensions={0} | concatenate | bytes 2097152 | tf_op jit(solution)/shard_map/jit(_roll_dynamic)/concatenate | solution.py:23
  178.4 3.2 %convolution_bitcast_fusion = f32[32,16,32,2,16]{2,0,4,1,3:T(8,128)S(1)} fusion(bf16[32,16,32,2,16]{2,0,3,4,1:T(8,128)(2,1)} %concatenate.15, s32[]{:T(128)S(6)} %select_n.131, bf16[16,1,32,2]{2,0,1,3:T(8,128)(2,1)S(1)} %get-tuple-element.14, bf16[16,1,32,2]{2,0,1,3:T(8,128)(2,1)S(1)} %get-tuple-element.13), kind=kOutput, calls=%fused_computation.38 | convolution fusion | flops 33562624 | bytes 4198404 | tf_op jit(solution)/shard_map/jkcsz,jsxt->xkctz/dot_general | solution.py:118
  181.6 0.0 copy-start.4
  181.6 22.8 %fusion.12 = bf16[32,32,32,2,16]{2,1,4,0,3:T(8,128)(2,1)} fusion(f32[32,16,32,2,16]{2,0,4,1,3:T(8,128)S(1)} %convolution_bitcast_fusion, f32[16,1,32,2]{2,0,3,1:T(8,128)S(1)} %get-tuple-element.10, f32[16,1,32,2]{2,0,3,1:T(8,128)S(1)} %get-tuple-element.9), kind=kOutput, calls=%fused_computation.26 | convolution fusion | flops 403703808 | bytes 4202496 | tf_op jit(solution)/shard_map/xkcsz,ksyt->xyctz/dot_general | solution.py:121
  204.4 10.5 %copy.35 = bf16[32,32,32,2,16]{2,4,3,1,0:T(8,128)(2,1)} copy(bf16[32,32,32,2,16]{2,1,4,0,3:T(8,128)(2,1)} %fusion.12) | data formatting | bytes 4194304 | tf_op jit(solution)/shard_map/convert_element_type | solution.py:123
  214.9 14.5 %fusion.94 = (f32[32,32,128]{2,1,0:T(8,128)S(1)}, f32[32,32,32,128]{3,2,1,0:T(8,128)}) fusion(f32[32]{0:T(128)S(1)} %bitcast.164, f32[32,32,128,32]{2,3,1,0:T(8,128)} %fusion.13, bf16[32,32,32,32]{2,3,1,0:T(8,128)(2,1)} %bitcast.160, bf16[16,128]{1,0:T(8,128)(2,1)S(1)} %get-tuple-element.41, bf16[16,128]{1,0:T(8,128)(2,1)S(1)} %get-tuple-element.42), kind=kOutput, calls=%fused_computation.168 | convolution fusion | flops 285097984 | bytes 36184192 | tf_op jit(solution)/shard_map/dot_general | solution.py:124
  229.4 0.0 copy-start.1
  229.5 10.9 %multiply_reduce_fusion = f32[32,32,128]{2,1,0:T(8,128)S(1)} fusion(f32[32,32,32,128]{3,2,1,0:T(8,128)} %get-tuple-element.36, f32[32,32,128]{2,1,0:T(8,128)S(1)} %broadcast_multiply_fusion), kind=kLoop, calls=%fused_computation.23 | loop fusion | flops 12451840 | bytes 17825792 | tf_op jit(solution)/shard_map/reduce_sum | solution.py:79
  240.4 0.1 add_rsqrt_fusion
  240.5 0.0 copy-done.2
  240.5 0.0 copy-done.3
  240.5 41.4 %fusion.21 = bf16[1,32,32,32,128]{4,3,2,1,0:T(8,128)(2,1)} fusion(f32[32]{0:T(128)S(1)} %bitcast.162, f32[32]{0:T(128)S(1)} %bitcast.163, f32[32,32,128]{2,1,0:T(8,128)S(1)} %add_rsqrt_fusion, f32[32,32,32,128]{3,2,1,0:T(8,128)} %get-tuple-element.36, f32[32,32,128]{2,1,0:T(8,128)S(1)} %broadcast_multiply_fusion), kind=kLoop, calls=%fused_computation.36 | loop fusion | flops 289406976 | bytes 26214656 | tf_op jit(solution)/shard_map/broadcast_in_dim | solution.py:134
  (16 shorter events, 0.2 us)
Async XLA Ops:
  7.4 114.9 %copy-start = (bf16[1,32,32]{2,1,0:T(8,128)(2,1)S(1)}, bf16[1,32,32]{2,1,0:T(8,128)(2,1)}, u32[]{:S(2)}) copy-start(bf16[1,32,32]{2,1,0:T(8,128)(2,1)} %param.8) | copy-start | bytes 6148
  7.4 69.8 %reduce-scatter.3.cloned.1.call-start = ((), (), s32[]{:S(2)}) async-start(), calls=%async_computation.2 | async-start | bytes 5242880 | tf_op jit(solution)/shard_map/reduce_scatter | solution.py:105
  29.7 61.4 %all-gather.3.cloned.1.call-start = ((), (), s32[]{:S(2)}) async-start(), calls=%async_computation.4 | async-start | bytes 6291456 | tf_op jit(solution)/shard_map/all_gather | solution.py:113
  30.3 72.8 %reduce-scatter.5.cloned.1.call-start = ((), (), s32[]{:S(2)}) async-start(), calls=%async_computation.3 | async-start | bytes 655360 | tf_op jit(solution)/shard_map/reduce_scatter | solution.py:109
  120.5 16.2 %collective-permute-start = (bf16[4,16,32,2,16]{2,0,3,4,1:T(4,128)(2,1)S(1)}, bf16[4,16,32,2,16]{2,0,3,4,1:T(4,128)(2,1)S(1)}, u32[]{:S(2)}, u32[]{:S(2)}) collective-permute-start(bf16[4,16,32,2,16]{2,0,3,4,1:T(4,128)(2,1)S(1)} %copy.30), channel_id=1, source_target_pairs={{0,8},{8,16},{16,24},{24,0},{1,9},{9,17},{17,25},{25,1},{2,10},{10... | collective-permute-start | bytes 393224 | tf_op jit(solution)/shard_map/ppermute | solution.py:20
  136.7 15.1 %collective-permute-start.1 = (bf16[4,16,32,2,16]{2,0,3,4,1:T(4,128)(2,1)S(1)}, bf16[4,16,32,2,16]{2,0,3,4,1:T(4,128)(2,1)S(1)}, u32[]{:S(2)}, u32[]{:S(2)}) collective-permute-start(bf16[4,16,32,2,16]{2,0,3,4,1:T(4,128)(2,1)S(1)} %collective-permute-done), channel_id=1, source_target_pairs={{0,8},{8,16},{16,24},{24,0},{1,9},{9,17},{17,25},{25,1},{2,10},{10... | collective-permute-start | bytes 393224 | tf_op jit(solution)/shard_map/ppermute | solution.py:20
  151.8 14.3 %collective-permute-start.2 = (bf16[4,16,32,2,16]{2,0,3,4,1:T(4,128)(2,1)S(1)}, bf16[4,16,32,2,16]{2,0,3,4,1:T(4,128)(2,1)S(1)}, u32[]{:S(2)}, u32[]{:S(2)}) collective-permute-start(bf16[4,16,32,2,16]{2,0,3,4,1:T(4,128)(2,1)S(1)} %collective-permute-done.1), channel_id=1, source_target_pairs={{0,8},{8,16},{16,24},{24,0},{1,9},{9,17},{17,25},{25,1},{2,10},{10... | collective-permute-start | bytes 393224 | tf_op jit(solution)/shard_map/ppermute | solution.py:20
  181.6 33.3 %copy-start.4 = (f32[1,32]{1,0:T(1,128)S(1)}, f32[1,32]{1,0:T(1,128)}, u32[]{:S(2)}) copy-start(f32[1,32]{1,0:T(1,128)} %param.9) | copy-start | bytes 388
  229.4 11.1 %copy-start.2 = (f32[1,32]{1,0:T(1,128)S(1)}, f32[1,32]{1,0:T(1,128)}, u32[]{:S(2)}) copy-start(f32[1,32]{1,0:T(1,128)} %param.11) | copy-start | bytes 388
  229.4 11.1 %copy-start.3 = (f32[1,32]{1,0:T(1,128)S(1)}, f32[1,32]{1,0:T(1,128)}, u32[]{:S(2)}) copy-start(f32[1,32]{1,0:T(1,128)} %param.10) | copy-start | bytes 388
  229.4 52.5 %copy-start.1 = (bf16[1,32,32]{2,1,0:T(8,128)(2,1)S(1)}, bf16[1,32,32]{2,1,0:T(8,128)(2,1)}, u32[]{:S(2)}) copy-start(bf16[1,32,32]{2,1,0:T(8,128)(2,1)} %param.8) | copy-start | bytes 6148
Sparse Core Ops, SparseCore 0:
  29.9 47.2 reduce-scatter.2
  80.2 21.8 reduce-scatter.4
Sparse Core Ops, SparseCore 1:
  31.8 59.3 all-gather.2
